TPU v7x, 32 devices: a whole 2x2x4 slice. The times are simulated.
32 devices in a mesh: row: 8 (over y, x, core), col: 4 (over z).
Axes of the slice: x: 2, y: 2, z: 4, core: 2. Of those that a mesh axis runs over, the one named last changes fastest.
Arguments:
- surface: bfloat16 [16384, 16384], P('row', 'col'), may hold values from -0.0234375 to 0.0234375
- excitation: float32 [16384, 128], P(('row', 'col')), may hold values from -6 to 6
- dtn_blocks: bfloat16 [32, 1024, 1024], P(('row', 'col')), may hold values from -0.09375 to 0.09375
- interp_blocks: bfloat16 [32, 1024, 2048], P(('row', 'col')), may hold values from -0.09375 to 0.09375
- adjacency: int32 [32, 6], P(('row', 'col')), may hold values from 0 to 31, as said below
Outputs:
- solution: float32 [16384, 128], P(('row', 'col'))
- residual: float32 [16384, 128], P(('row', 'col'))
Inputs may be any that keep to these rules, and one draw needn't show every extreme that they name: `adjacency`: entry [s, k] names a subdomain of the same spatial group as s (equal index // 4); it may name s itself, which adds nothing.
All inputs are finite; a program needn't handle non-finite values.
Results may differ from a plain program's by a relative error of at most 0.02.
Values may be sent and summed in bfloat16 or wider, within the bound.
A program may use at most 64 MiB of HBM per device.

v0:
```python
import jax
import jax.numpy as jnp
from jax import lax
from jax.sharding import PartitionSpec as P

ITERS = 2
NADJ = 6
damping = 0.25
face_weight = 0.25


def broadcast(value, axis, source):
    kept = jnp.where(lax.axis_index(axis) == source, value, 0).astype(value.dtype)
    return lax.psum(kept, axis)


def local(surface, excitation, dtn_blocks, interp_blocks, adjacency):
    col_count = lax.axis_size("col")
    row_count = lax.axis_size("row")
    col_index = lax.axis_index("col")
    dtn_block = dtn_blocks[0]
    interp_block = interp_blocks[0]
    local_adjacent = adjacency[0] % col_count
    current = excitation
    residual = excitation
    for sweep in range(ITERS):
        rounded = current.astype(jnp.bfloat16)
        group_block = lax.all_gather(rounded, "col", axis=0, tiled=True)
        per_column = row_count // col_count
        received = [
            broadcast(group_block, "row", col_index * per_column + member)
            for member in range(per_column)
        ]
        column_block = jnp.concatenate(received, axis=0)
        traces = jnp.dot(interp_block, group_block, preferred_element_type=jnp.float32).astype(
            jnp.bfloat16
        )
        segment = lax.all_gather(traces[None], "col", axis=0, tiled=True)
        owners = jnp.arange(segment.shape[0], dtype=jnp.int32)
        counts = jnp.sum((local_adjacent[None, :] == owners[:, None]).astype(jnp.float32), axis=1)
        neighbours = jnp.einsum(
            "p,pmn->mn", counts.astype(jnp.bfloat16), segment, preferred_element_type=jnp.float32
        )
        own_wide = traces.astype(jnp.float32)
        combined = jnp.dot(dtn_block, traces, preferred_element_type=jnp.float32) + own_wide
        combined = combined + face_weight * (NADJ * own_wide - neighbours)
        response = combined.astype(jnp.bfloat16)
        surface_part = jnp.dot(surface, column_block, preferred_element_type=jnp.float32)
        volume_part = lax.dot_general(
            interp_block, response, (((0,), (0,)), ((), ())), preferred_element_type=jnp.float32
        )
        summed = lax.psum_scatter(
            (surface_part + volume_part).astype(jnp.bfloat16),
            "col",
            scatter_dimension=0,
            tiled=True,
        ).astype(jnp.float32)
        residual = excitation - current - summed
        current = current + damping * residual
    return (current, residual)


def solution(mesh):
    in_specs = (
        P("row", "col"),
        P(("row", "col"), None),
        P(("row", "col"), None, None),
        P(("row", "col"), None, None),
        P(("row", "col"), None),
    )
    out_specs = (P(("row", "col"), None), P(("row", "col"), None))
    return jax.shard_map(local, mesh=mesh, in_specs=in_specs, out_specs=out_specs, check_vma=False)
```

profile of v0, /device:TPU:0, one launch (start us, length us, event | category | flops | bytes accessed | tf_op | source)
XLA Modules:
  0.0 250.6 jit_solution(15848962410064258992)
XLA Ops:
  8.0 0.0 all-reduce.7.cloned.1.call-start
  8.1 1.2 copy.18
  9.3 17.4 %all_gather.12 = bf16[2048,128]{0,1:T(8,128)(2,1)S(1)} all-gather(bf16[512,128]{0,1:T(8,128)(2,1)S(1)} %convert_element_type.58), channel_id=1, replica_groups=mesh['row'=8,'col'=4] {'col'}, dimensions={0}, use_global_device_ids=true | all-gather | bytes 655360 | tf_op jit(solution)/shard_map/all_gather | solution.py:28
  26.7 1.0 broadcast_select_fusion.3
  27.8 0.0 all-gather.5.cloned.1.call-start
  27.8 4.1 %fusion.54 = bf16[1024,128]{1,0:T(8,128)(2,1)} fusion(bf16[2048,128]{0,1:T(8,128)(2,1)S(1)} %all_gather.12, bf16[1,1024,2048]{2,1,0:T(8,128)(2,1)} %param.8), kind=kOutput, calls=%fused_computation.26 | convolution fusion | flops 537001984 | bytes 4980736 | tf_op jit(solution)/shard_map/dot_general | solution.py:35
  32.0 0.0 all-gather.5.cloned.1.call-update
  32.0 0.0 reduce-scatter.3.cloned.1.call-start
  32.1 0.1 convert_reduce_fusion
  32.2 54.3 %all-reduce.7.cloned.1.call-done = (bf16[2048,128]{0,1:T(8,128)(2,1)}, bf16[2048,128]{0,1:T(8,128)(2,1)}) async-done(((bf16[2048,128]{0,1:T(8,128)(2,1)}, bf16[2048,128]{0,1:T(8,128)(2,1)}), (bf16[2048,128]{0,1:T(8,128)(2,1)}, bf16[2048,128]{0,1:T(8,128)(2,1)})) %all-reduce.7.cloned.1.call-update) | async-done | bytes 1048592 | tf_op jit(solution)/shard_map/psum | solution.py:14
  86.4 11.8 %fusion.60 = f32[128,2048]{1,0:T(8,128)S(1)} fusion(bf16[2048,4096]{1,0:T(8,128)(2,1)} %param.5, bf16[2048,128]{0,1:T(8,128)(2,1)} %get-tuple-element.8, bf16[2048,128]{0,1:T(8,128)(2,1)} %get-tuple-element.9), kind=kOutput, calls=%fused_computation.28 | convolution fusion | flops 2149580800 | bytes 18874368 | tf_op jit(solution)/shard_map/dot_general | solution.py:48
  98.2 0.0 all-gather.5.cloned.1.call-done
  98.2 3.0 %fusion.70 = f32[1,1024,128]{2,0,1:T(1,128)} fusion(bf16[4,1024,128]{2,1,0:T(8,128)(2,1)} %bitcast.101, bf16[4]{0:T(256)(128)(2,1)S(1)} %convert_reduce_fusion), kind=kOutput, calls=%fused_computation.38 | convolution fusion | flops 1048576 | bytes 1572872 | tf_op jit(solution)/shard_map/p,pmn->mn/dot_general | solution.py:41
  101.2 4.6 %fusion.20 = bf16[2048,128]{0,1:T(8,128)(2,1)} fusion(f32[128,2048]{1,0:T(8,128)S(1)} %fusion.60, bf16[1,1024,2048]{2,1,0:T(8,128)(2,1)} %param.8, bf16[1024,128]{1,0:T(8,128)(2,1)} %fusion.54, bf16[1,1024,1024]{2,1,0:T(8,128)(2,1)S(1)} %copy-done, f32[1024,128]{1,0:T(8,128)} %bitcast.100), kind=kOutput, calls=%fused_computation.12 | convolution fusion | flops 806748160 | bytes 8650752 | tf_op jit(solution)/shard_map/dot_general | solution.py:49
  105.8 0.0 reduce-scatter.3.cloned.1.call-update
  105.8 0.0 all-reduce.5.cloned.1.call-start
  105.8 21.1 %reduce-scatter.3.cloned.1.call-done = bf16[512,128]{0,1:T(8,128)(2,1)} async-done(((bf16[2048,128]{0,1:T(8,128)(2,1)}), bf16[512,128]{0,1:T(8,128)(2,1)}) %reduce-scatter.3.cloned.1.call-update) | async-done | bytes 131088 | tf_op jit(solution)/shard_map/reduce_scatter | solution.py:52
  127.0 1.0 fusion.88
  127.9 15.3 %all_gather.14 = bf16[2048,128]{0,1:T(8,128)(2,1)S(1)} all-gather(bf16[512,128]{0,1:T(8,128)(2,1)S(1)} %fusion.88), channel_id=1, replica_groups=mesh['row'=8,'col'=4] {'col'}, dimensions={0}, use_global_device_ids=true | all-gather | bytes 655360 | tf_op jit(solution)/shard_map/all_gather | solution.py:28
  143.2 1.0 broadcast_select_fusion.2
  144.3 0.0 all-gather.7.cloned.1.call-start
  144.3 4.1 %fusion.57 = bf16[128,1024]{0,1:T(8,128)(2,1)} fusion(bf16[2048,128]{0,1:T(8,128)(2,1)S(1)} %all_gather.14, bf16[1,1024,2048]{2,1,0:T(8,128)(2,1)} %param.8), kind=kOutput, calls=%fused_computation.27 | convolution fusion | flops 537001984 | bytes 4980736 | tf_op jit(solution)/shard_map/dot_general | solution.py:35
  148.5 0.2 reduce-scatter.5.cloned.1.call-start
  148.7 51.0 %all-reduce.5.cloned.1.call-done = (bf16[2048,128]{0,1:T(8,128)(2,1)}, bf16[2048,128]{0,1:T(8,128)(2,1)}) async-done(((bf16[2048,128]{0,1:T(8,128)(2,1)}, bf16[2048,128]{0,1:T(8,128)(2,1)}), (bf16[2048,128]{0,1:T(8,128)(2,1)}, bf16[2048,128]{0,1:T(8,128)(2,1)})) %all-reduce.5.cloned.1.call-update) | async-done | bytes 1048592 | tf_op jit(solution)/shard_map/psum | solution.py:14
  199.7 11.8 %fusion.64 = f32[128,2048]{1,0:T(8,128)S(1)} fusion(bf16[2048,4096]{1,0:T(8,128)(2,1)} %param.5, bf16[2048,128]{0,1:T(8,128)(2,1)} %get-tuple-element.6, bf16[2048,128]{0,1:T(8,128)(2,1)} %get-tuple-element.7), kind=kOutput, calls=%fused_computation.32 | convolution fusion | flops 2149580800 | bytes 18874368 | tf_op jit(solution)/shard_map/dot_general | solution.py:48
  211.5 0.0 all-gather.7.cloned.1.call-done
  211.5 3.0 %fusion.68 = f32[1,1024,128]{2,0,1:T(1,128)} fusion(bf16[4,1024,128]{2,1,0:T(8,128)(2,1)} %bitcast.102, bf16[4]{0:T(256)(128)(2,1)S(1)} %convert_reduce_fusion), kind=kOutput, calls=%fused_computation.36 | convolution fusion | flops 1048576 | bytes 1572872 | tf_op jit(solution)/shard_map/p,pmn->mn/dot_general | solution.py:41
  214.5 4.6 %fusion.23 = bf16[2048,128]{0,1:T(8,128)(2,1)} fusion(f32[128,2048]{1,0:T(8,128)S(1)} %fusion.64, bf16[1,1024,2048]{2,1,0:T(8,128)(2,1)} %param.8, bf16[128,1024]{0,1:T(8,128)(2,1)} %fusion.57, bf16[1,1024,1024]{2,1,0:T(8,128)(2,1)S(1)} %copy-done, f32[1024,128]{1,0:T(8,128)} %bitcast.99), kind=kOutput, calls=%fused_computation.13 | convolution fusion | flops 806748160 | bytes 8650752 | tf_op jit(solution)/shard_map/dot_general | solution.py:49
  219.1 21.2 %reduce-scatter.5.cloned.1.call-done = bf16[512,128]{0,1:T(8,128)(2,1)} async-done(((bf16[2048,128]{0,1:T(8,128)(2,1)}), bf16[512,128]{0,1:T(8,128)(2,1)}) %reduce-scatter.5.cloned.1.call-update) | async-done | bytes 131088 | tf_op jit(solution)/shard_map/reduce_scatter | solution.py:52
  240.3 1.0 convert_subtract_fusion
  241.3 0.8 copy.22
  242.1 0.8 copy.21
  (12 shorter events, 0.1 us)
Async XLA Ops:
  8.0 93.2 %copy-start = (bf16[1,1024,1024]{2,1,0:T(8,128)(2,1)S(1)}, bf16[1,1024,1024]{2,1,0:T(8,128)(2,1)}, u32[]{:S(2)}) copy-start(bf16[1,1024,1024]{2,1,0:T(8,128)(2,1)} %param.7) | copy-start | bytes 6291460
  8.0 78.4 %all-reduce.7.cloned.1.call-start = ((), (), s32[]{:S(2)}) async-start(), calls=%async_computation.7 | async-start | bytes 2097152 | tf_op jit(solution)/shard_map/psum | solution.py:14
  27.7 4.3 %copy-start.2 = (s32[1,6]{1,0:T(1,128)S(1)}, s32[1,6]{1,0:T(1,128)}, u32[]{:S(2)}) copy-start(s32[1,6]{1,0:T(1,128)} %param.9) | copy-start | bytes 76
  27.8 70.5 %all-gather.5.cloned.1.call-start = ((), (), s32[]{:S(2)}) async-start(), calls=%async_computation.4 | async-start | bytes 1310720 | tf_op jit(solution)/shard_map/all_gather | solution.py:38
  32.0 95.0 %reduce-scatter.3.cloned.1.call-start = ((), (), s32[]{:S(2)}) async-start(), calls=%async_computation.2 | async-start | bytes 655360 | tf_op jit(solution)/shard_map/reduce_scatter | solution.py:52
  105.8 93.9 %all-reduce.5.cloned.1.call-start = ((), (), s32[]{:S(2)}) async-start(), calls=%async_computation.6 | async-start | bytes 2097152 | tf_op jit(solution)/shard_map/psum | solution.py:14
  144.3 67.2 %all-gather.7.cloned.1.call-start = ((), (), s32[]{:S(2)}) async-start(), calls=%async_computation.5 | async-start | bytes 1310720 | tf_op jit(solution)/shard_map/all_gather | solution.py:38
  148.5 91.8 %reduce-scatter.5.cloned.1.call-start = ((), (), s32[]{:S(2)}) async-start(), calls=%async_computation.3 | async-start | bytes 655360 | tf_op jit(solution)/shard_map/reduce_scatter | solution.py:52
  214.5 25.8 %copy-start.1 = (bf16[512,128]{0,1:T(8,128)(2,1)S(1)}, bf16[512,128]{0,1:T(8,128)(2,1)}, u32[]{:S(2)}) copy-start(bf16[512,128]{0,1:T(8,128)(2,1)} %reduce-scatter.3.cloned.1.call-done) | copy-start | bytes 393220
Sparse Core Ops, SparseCore 0:
  27.9 58.5 all-reduce.6
  144.4 55.2 all-reduce.4
Sparse Core Ops, SparseCore 1:
  32.1 29.6 all-gather.4
  105.9 21.0 reduce-scatter.2
  148.6 26.4 all-gather.6
  219.2 21.0 reduce-scatter.4
where the time goes:
time: 251 us
  waiting for transfers between devices  148 us (59%)
  matrix products  46.9 us (19%)
  blocking collectives  32.7 us (13%)
  between operations  15.8 us (6%)
  other arithmetic  4.18 us (2%)
  local copies, waits for them, and re-layouts  2.9 us (1%)
    psum x2, waiting for transfers between devices, broadcast(): return lax.psum(kept, axis)  105 us
    reduce_scatter x2, waiting for transfers between devices, local(): lax.psum_scatter((surface_part + volume_part).astype(jnp.bfloat16), 'col'...  42.3 us
    all_gather x2, blocking collectives, local(): group_block = lax.all_gather(rounded, 'col', axis=0, tiled=True)  32.7 us
    dot_general x2, matrix products, local(): jnp.dot(surface, column_block, preferred_element_type=jnp.float32)  23.5 us
    dot_general x2, matrix products, local(): lax.dot_general(interp_block, response, (((0,), (0,)), ((), ())), preferr...  9.18 us
    dot_general x2, matrix products, local(): jnp.dot(interp_block, group_block, preferred_element_type=jnp.float32)  8.29 us
    dot_general x2, matrix products, local(): jnp.einsum('p,pmn->mn', counts.astype(jnp.bfloat16), segment, preferred_e...  5.92 us
  transfers between devices with their start and end apart: 6, of which 4 were waited for; matrix products, arithmetic and copies ran while one was open for 13% of the time, Pallas kernels for 0%

commit v1 on v0

--- a/solution.py
+++ b/solution.py
@@ -25,7 +25,9 @@
     residual = excitation
     for sweep in range(ITERS):
         rounded = current.astype(jnp.bfloat16)
-        group_block = lax.all_gather(rounded, "col", axis=0, tiled=True)
+        group_block = jnp.concatenate(
+            lax.all_to_all(jnp.stack([rounded] * lax.axis_size("col")), "col", 0, 0), axis=0
+        )
         per_column = row_count // col_count
         received = [
             broadcast(group_block, "row", col_index * per_column + member)

time: 251 us -> 254 us (1.012)
  blocking collectives: 32.7 us -> 15.5 us
  waiting for transfers between devices: 148 us -> 159 us
  starting transfers between devices: 0.44 us -> 6.75 us
    all_gather x2 -> x0, blocking collectives: 32.7 us -> none  [local(): group_block = lax.all_gather(rounded, 'col', axis=0, tiled=True)]
    all_to_all x0 -> x1, blocking collectives: none -> 15.5 us  [local(): lax.all_to_all(jnp.stack([rounded] * lax.axis_size('col')), 'col', 0, 0)]
    all_to_all x0 -> x1, waiting for transfers between devices: none -> 14.5 us  [local(): lax.all_to_all(jnp.stack([rounded] * lax.axis_size('col')), 'col', 0, 0)]
    all_to_all x0 -> x1, starting transfers between devices: none -> 6.35 us  [local(): lax.all_to_all(jnp.stack([rounded] * lax.axis_size('col')), 'col', 0, 0)]
  transfers between devices with their start and end apart: 6 -> 7, of which waited for: 4 -> 5; matrix products, arithmetic and copies ran while one was open for 13% -> 13% of each run, Pallas kernels for 0% -> 0%
where the time goes in v1:
time: 254 us; the launch traced here: 253 us
  waiting for transfers between devices  159 us (63%)
  matrix products  46.9 us (18%)
  between operations  15.8 us (6%)
  blocking collectives  15.5 us (6%)
  starting transfers between devices  6.75 us (3%)
  other arithmetic  5.33 us (2%)
  local copies, waits for them, and re-layouts  3.82 us (2%)
    psum x2, waiting for transfers between devices, broadcast(): return lax.psum(kept, axis)  103 us
    reduce_scatter x2, waiting for transfers between devices, local(): lax.psum_scatter((surface_part + volume_part).astype(jnp.bfloat16), 'col'...  41.2 us
    dot_general x2, matrix products, local(): jnp.dot(surface, column_block, preferred_element_type=jnp.float32)  23.7 us
    all_to_all x1, blocking collectives, local(): lax.all_to_all(jnp.stack([rounded] * lax.axis_size('col')), 'col', 0, 0)  15.5 us
    all_to_all x1, waiting for transfers between devices, local(): lax.all_to_all(jnp.stack([rounded] * lax.axis_size('col')), 'col', 0, 0)  14.5 us
    dot_general x2, matrix products, local(): lax.dot_general(interp_block, response, (((0,), (0,)), ((), ())), preferr...  9.01 us
    dot_general x2, matrix products, local(): jnp.dot(interp_block, group_block, preferred_element_type=jnp.float32)  8.28 us
    all_to_all x1, starting transfers between devices, local(): lax.all_to_all(jnp.stack([rounded] * lax.axis_size('col')), 'col', 0, 0)  6.35 us
  transfers between devices with their start and end apart: 7, of which 5 were waited for; matrix products, arithmetic and copies ran while one was open for 13% of the time, Pallas kernels for 0%

profile of v1, /device:TPU:0, one launch (start us, length us, event | category | flops | bytes accessed | tf_op | source)
XLA Modules:
  0.0 253.1 jit_solution(8476664744811565601)
XLA Ops:
  8.0 1.1 convert_element_type.58
  9.1 0.9 stack.4
  10.0 6.3 %all-to-all-start = ((bf16[4,512,128]{2,1,0:T(8,128)(2,1)}), bf16[4,512,128]{2,1,0:T(8,128)(2,1)S(1)}, u32[]{:S(2)}, u32[]{:S(2)}) async-start(bf16[4,512,128]{2,1,0:T(8,128)(2,1)} %stack.4), calls=%async_computation | async-start | bytes 1048576 | tf_op jit(solution)/shard_map/all_to_all | solution.py:29
  16.3 14.5 %all-to-all-done = bf16[4,512,128]{2,1,0:T(8,128)(2,1)S(1)} async-done(((bf16[4,512,128]{2,1,0:T(8,128)(2,1)}), bf16[4,512,128]{2,1,0:T(8,128)(2,1)S(1)}, u32[]{:S(2)}, u32[]{:S(2)}) %all-to-all-start) | async-done | bytes 524320 | tf_op jit(solution)/shard_map/all_to_all | solution.py:29
  30.8 1.1 broadcast_select_fusion.3
  31.9 0.0 all-gather.5.cloned.1.call-start
  32.0 4.1 %fusion.54 = bf16[1024,128]{1,0:T(8,128)(2,1)} fusion(bf16[2048,128]{1,0:T(8,128)(2,1)S(1)} %bitcast.104, bf16[1,1024,2048]{2,1,0:T(8,128)(2,1)} %param.8), kind=kOutput, calls=%fused_computation.26 | convolution fusion | flops 537001984 | bytes 4980736 | tf_op jit(solution)/shard_map/dot_general | solution.py:37
  36.1 0.0 reduce-scatter.3.cloned.1.call-start
  36.2 0.1 convert_reduce_fusion
  36.3 51.6 %all-reduce.7.cloned.1.call-done = (bf16[2048,128]{1,0:T(8,128)(2,1)}, bf16[2048,128]{1,0:T(8,128)(2,1)}) async-done(((bf16[2048,128]{1,0:T(8,128)(2,1)}, bf16[2048,128]{1,0:T(8,128)(2,1)}), (bf16[2048,128]{1,0:T(8,128)(2,1)}, bf16[2048,128]{1,0:T(8,128)(2,1)})) %all-reduce.7.cloned.1.call-update) | async-done | bytes 1048592 | tf_op jit(solution)/shard_map/psum | solution.py:14
  88.0 11.9 %fusion.60 = f32[128,2048]{1,0:T(8,128)S(1)} fusion(bf16[2048,4096]{1,0:T(8,128)(2,1)} %param.5, bf16[2048,128]{1,0:T(8,128)(2,1)} %get-tuple-element.8, bf16[2048,128]{1,0:T(8,128)(2,1)} %get-tuple-element.9), kind=kOutput, calls=%fused_computation.28 | convolution fusion | flops 2149580800 | bytes 18874368 | tf_op jit(solution)/shard_map/dot_general | solution.py:50
  99.9 2.9 %fusion.70 = f32[1,1024,128]{2,0,1:T(1,128)} fusion(bf16[4,1024,128]{2,1,0:T(8,128)(2,1)} %bitcast.109, bf16[4]{0:T(256)(128)(2,1)S(1)} %convert_reduce_fusion), kind=kOutput, calls=%fused_computation.38 | convolution fusion | flops 1048576 | bytes 1572872 | tf_op jit(solution)/shard_map/p,pmn->mn/dot_general | solution.py:43
  102.8 4.4 %fusion.20 = bf16[2048,128]{0,1:T(8,128)(2,1)} fusion(f32[128,2048]{1,0:T(8,128)S(1)} %fusion.60, bf16[1,1024,2048]{2,1,0:T(8,128)(2,1)} %param.8, bf16[1024,128]{1,0:T(8,128)(2,1)S(1)} %copy-done.1, bf16[1,1024,1024]{2,1,0:T(8,128)(2,1)S(1)} %copy-done, f32[1024,128]{1,0:T(8,128)} %bitcast.108), kind=kOutput, calls=%fused_computation.12 | convolution fusion | flops 806748160 | bytes 8650752 | tf_op jit(solution)/shard_map/dot_general | solution.py:51
  107.2 0.0 all-reduce.5.cloned.1.call-start
  107.3 1.1 copy.17
  108.4 20.0 %reduce-scatter.3.cloned.1.call-done = bf16[512,128]{0,1:T(8,128)(2,1)} async-done(((bf16[2048,128]{0,1:T(8,128)(2,1)}), bf16[512,128]{0,1:T(8,128)(2,1)}) %reduce-scatter.3.cloned.1.call-update) | async-done | bytes 131088 | tf_op jit(solution)/shard_map/reduce_scatter | solution.py:54
  128.4 1.0 fusion.88
  129.3 0.1 copy.19
  129.5 0.1 stack.5
  129.6 15.5 %all_to_all.10 = bf16[4,512,128]{2,1,0:T(8,128)(2,1)S(1)} all-to-all(bf16[4,512,128]{2,1,0:T(8,128)(2,1)S(1)} %stack.5), channel_id=1, replica_groups=mesh['row'=8,'col'=4] {'col'}, dimensions={0} | all-to-all | bytes 1048576 | tf_op jit(solution)/shard_map/all_to_all | solution.py:29
  145.1 1.1 broadcast_select_fusion.2
  146.2 0.0 all-gather.7.cloned.1.call-start
  146.2 4.1 %fusion.57 = bf16[128,1024]{0,1:T(8,128)(2,1)} fusion(bf16[2048,128]{1,0:T(8,128)(2,1)S(1)} %bitcast.105, bf16[1,1024,2048]{2,1,0:T(8,128)(2,1)} %param.8), kind=kOutput, calls=%fused_computation.27 | convolution fusion | flops 537001984 | bytes 4980736 | tf_op jit(solution)/shard_map/dot_general | solution.py:37
  150.4 0.2 reduce-scatter.5.cloned.1.call-start
  150.6 51.5 %all-reduce.5.cloned.1.call-done = (bf16[2048,128]{1,0:T(8,128)(2,1)}, bf16[2048,128]{1,0:T(8,128)(2,1)}) async-done(((bf16[2048,128]{1,0:T(8,128)(2,1)}, bf16[2048,128]{1,0:T(8,128)(2,1)}), (bf16[2048,128]{1,0:T(8,128)(2,1)}, bf16[2048,128]{1,0:T(8,128)(2,1)})) %all-reduce.5.cloned.1.call-update) | async-done | bytes 1048592 | tf_op jit(solution)/shard_map/psum | solution.py:14
  202.2 11.8 %fusion.64 = f32[128,2048]{1,0:T(8,128)S(1)} fusion(bf16[2048,4096]{1,0:T(8,128)(2,1)} %param.5, bf16[2048,128]{1,0:T(8,128)(2,1)} %get-tuple-element.6, bf16[2048,128]{1,0:T(8,128)(2,1)} %get-tuple-element.7), kind=kOutput, calls=%fused_computation.32 | convolution fusion | flops 2149580800 | bytes 18874368 | tf_op jit(solution)/shard_map/dot_general | solution.py:50
  214.0 3.0 %fusion.68 = f32[1,1024,128]{2,0,1:T(1,128)} fusion(bf16[4,1024,128]{2,1,0:T(8,128)(2,1)} %bitcast.110, bf16[4]{0:T(256)(128)(2,1)S(1)} %convert_reduce_fusion), kind=kOutput, calls=%fused_computation.36 | convolution fusion | flops 1048576 | bytes 1572872 | tf_op jit(solution)/shard_map/p,pmn->mn/dot_general | solution.py:43
  217.0 4.6 %fusion.23 = bf16[2048,128]{0,1:T(8,128)(2,1)} fusion(f32[128,2048]{1,0:T(8,128)S(1)} %fusion.64, bf16[1,1024,2048]{2,1,0:T(8,128)(2,1)} %param.8, bf16[128,1024]{0,1:T(8,128)(2,1)} %fusion.57, bf16[1,1024,1024]{2,1,0:T(8,128)(2,1)S(1)} %copy-done, f32[1024,128]{1,0:T(8,128)} %bitcast.107), kind=kOutput, calls=%fused_computation.13 | convolution fusion | flops 806748160 | bytes 8650752 | tf_op jit(solution)/shard_map/dot_general | solution.py:51
  221.6 21.2 %reduce-scatter.5.cloned.1.call-done = bf16[512,128]{0,1:T(8,128)(2,1)} async-done(((bf16[2048,128]{0,1:T(8,128)(2,1)}), bf16[512,128]{0,1:T(8,128)(2,1)}) %reduce-scatter.5.cloned.1.call-update) | async-done | bytes 131088 | tf_op jit(solution)/shard_map/reduce_scatter | solution.py:54
  242.8 1.0 convert_subtract_fusion
  243.8 0.8 copy.22
  244.6 0.8 copy.21
  (18 shorter events, 0.2 us)
Async XLA Ops:
  8.0 94.8 %copy-start = (bf16[1,1024,1024]{2,1,0:T(8,128)(2,1)S(1)}, bf16[1,1024,1024]{2,1,0:T(8,128)(2,1)}, u32[]{:S(2)}) copy-start(bf16[1,1024,1024]{2,1,0:T(8,128)(2,1)} %param.7) | copy-start | bytes 6291460
  10.0 20.8 %all-to-all-start = ((bf16[4,512,128]{2,1,0:T(8,128)(2,1)}), bf16[4,512,128]{2,1,0:T(8,128)(2,1)S(1)}, u32[]{:S(2)}, u32[]{:S(2)}) async-start(bf16[4,512,128]{2,1,0:T(8,128)(2,1)} %stack.4), calls=%async_computation | async-start | bytes 1048576 | tf_op jit(solution)/shard_map/all_to_all | solution.py:29
  16.3 71.6 %all-reduce.7.cloned.1.call-start = ((), (), s32[]{:S(2)}) async-start(), calls=%async_computation.9 | async-start | bytes 2097152 | tf_op jit(solution)/shard_map/psum | solution.py:14
  31.9 4.3 %copy-start.3 = (s32[1,6]{1,0:T(1,128)S(1)}, s32[1,6]{1,0:T(1,128)}, u32[]{:S(2)}) copy-start(s32[1,6]{1,0:T(1,128)} %param.9) | copy-start | bytes 76
  31.9 67.9 %all-gather.5.cloned.1.call-start = ((), (), s32[]{:S(2)}) async-start(), calls=%async_computation.6 | async-start | bytes 1310720 | tf_op jit(solution)/shard_map/all_gather | solution.py:40
  36.1 92.2 %reduce-scatter.3.cloned.1.call-start = ((), (), s32[]{:S(2)}) async-start(), calls=%async_computation.4 | async-start | bytes 655360 | tf_op jit(solution)/shard_map/reduce_scatter | solution.py:54
  87.9 14.9 %copy-start.1 = (bf16[1024,128]{1,0:T(8,128)(2,1)S(1)}, bf16[1024,128]{1,0:T(8,128)(2,1)}, u32[]{:S(2)}) copy-start(bf16[1024,128]{1,0:T(8,128)(2,1)} %fusion.54) | copy-start | bytes 786436
  107.2 94.9 %all-reduce.5.cloned.1.call-start = ((), (), s32[]{:S(2)}) async-start(), calls=%async_computation.8 | async-start | bytes 2097152 | tf_op jit(solution)/shard_map/psum | solution.py:14
  146.2 67.8 %all-gather.7.cloned.1.call-start = ((), (), s32[]{:S(2)}) async-start(), calls=%async_computation.7 | async-start | bytes 1310720 | tf_op jit(solution)/shard_map/all_gather | solution.py:40
  150.4 92.4 %reduce-scatter.5.cloned.1.call-start = ((), (), s32[]{:S(2)}) async-start(), calls=%async_computation.5 | async-start | bytes 655360 | tf_op jit(solution)/shard_map/reduce_scatter | solution.py:54
  217.0 25.8 %copy-start.2 = (bf16[512,128]{0,1:T(8,128)(2,1)S(1)}, bf16[512,128]{0,1:T(8,128)(2,1)}, u32[]{:S(2)}) copy-start(bf16[512,128]{0,1:T(8,128)(2,1)} %reduce-scatter.3.cloned.1.call-done) | copy-start | bytes 393220
Sparse Core Ops, SparseCore 0:
  32.0 55.8 all-reduce.6
  146.3 55.8 all-reduce.4
Sparse Core Ops, SparseCore 1:
  36.2 27.0 all-gather.4
  107.3 21.0 reduce-scatter.2
  150.5 26.9 all-gather.6
  221.7 21.0 reduce-scatter.4
